TPU v7x, 32 devices: a whole 2x2x4 slice. The times are simulated.
32 devices in a mesh: face: 8 (over z, y), col: 4 (over x, core).
Axes of the slice: x: 2, y: 2, z: 4, core: 2. Of those that a mesh axis runs over, the one named last changes fastest.
Arguments:
- fields: float32 [4, 160, 80, 128], P(None, 'face', 'col'), may hold values from -6 to 6
- metric_diag: float32 [2, 160, 80], P(None, 'face', 'col'), may hold values from 0.05 to 0.5
- metric_cross: float32 [160, 80], P('face', 'col'), may hold values from -0.1 to 0.1
- point_mass: float32 [160, 80], P('face', 'col'), may hold values from 0.5 to 2
Outputs:
- biharmonic: float32 [4, 160, 80, 128], P(None, 'face', 'col')
All inputs are finite; a program needn't handle non-finite values.
Results may differ from a plain program's by a relative error of at most 0.00024.
Values sent between devices are 32-bit elements; how exact they have to be, the bound alone decides.
A program may use at most 64 MiB of HBM per device.

v0:
```python
import functools

import jax
import jax.numpy as jnp
import numpy as np
from jax import lax
from jax.experimental import pallas as pl
from jax.experimental.pallas import tpu as pltpu
from jax.sharding import PartitionSpec as P

MESH = pl.DeviceIdType.MESH


def derivative_table():
    small = 1.0 / np.sqrt(5.0)
    nodes = np.array([-1.0, -small, small, 1.0])
    count = nodes.shape[0]
    weights = np.array(
        [np.prod([nodes[a] - nodes[k] for k in range(count) if k != a]) for a in range(count)]
    )
    table = np.zeros((count, count))
    for a in range(count):
        for b in range(count):
            if a == b:
                table[a, b] = np.sum([1.0 / (nodes[a] - nodes[k]) for k in range(count) if k != a])
            else:
                table[a, b] = weights[a] / weights[b] / (nodes[a] - nodes[b])
    return [[float(np.float32(v)) for v in row] for row in table]


def dot4(coefs, terms):
    total = None
    for c, t in zip(coefs, terms):
        if isinstance(c, float) and c == 0.0:
            continue
        total = c * t if total is None else total + c * t
    return total


def kernel(
    faces, cols, nf, nbx, nby,
    fields_hbm, diag_ref, cross_ref, mass_ref, out_ref,
    raw, U, M, W, T, spread, rM,
    sC1, rR1, rC1, rK1, sC2, rR2, rC2, rK2,
    load_sem, mass_send, mass_recv, send_sem, recv_sem,
):
    face, col = lax.axis_index("face"), lax.axis_index("col")
    fside = (lax.rem(face + faces - 1, faces), lax.rem(face + 1, faces))
    cside = (lax.rem(col + cols - 1, cols), lax.rem(col + 1, cols))
    peers = [(fside[0], col), (fside[1], col), (face, cside[0]), (face, cside[1])]
    peers += [(fside[s], cside[t]) for s in range(2) for t in range(2)]
    opposite = [1, 0, 3, 2, 7, 6, 5, 4]

    nx, ny, nq = 4 * nbx, 4 * nby, 2 * nby
    lanes = raw.shape[-1]
    order = [0, nbx - 1] + list(range(1, nbx - 1))
    loads = {
        ex: pltpu.make_async_copy(
            fields_hbm.at[pl.ds(4 * ex, 4)], raw.at[pl.ds(4 * ex, 4)], load_sem.at[ex]
        )
        for ex in order
    }
    for ex in order:
        loads[ex].start()
    barrier = pltpu.get_barrier_semaphore()
    for peer in peers:
        pl.semaphore_signal(barrier, inc=1, device_id=peer, device_id_type=MESH)

    D = derivative_table()
    sub = lax.broadcasted_iota(jnp.int32, (2 * nf, lanes), 0)
    is_low = sub < nf
    low = jnp.where(is_low, 1.0, 0.0)
    high = 1.0 - low

    def swap(v):
        return pltpu.roll(v, nf, 0)

    def halves(table):
        return [
            [
                jnp.where(is_low, table[2 * p][2 * q + k], table[2 * p + 1][2 * q + 1 - k])
                for q in range(2) for k in range(2)
            ]
            for p in range(2)
        ]

    minus_t = [[-D[b][a] for b in range(4)] for a in range(4)]
    D_half, minus_half = halves(D), halves(minus_t)

    row = lax.broadcasted_iota(jnp.int32, (nf * ny, 3 * ny), 0)
    lane = lax.broadcasted_iota(jnp.int32, (nf * ny, 3 * ny), 1)
    keep = jnp.zeros((nf * ny, 3 * ny), jnp.float32)
    for k in range(3):
        first_row = nf * (lane - k * ny)
        keep = jnp.where((row >= first_row) & (row < first_row + nf), 1.0, keep)
    ones = jnp.ones((3 * ny, lanes), jnp.bfloat16)

    def split(slot, m):
        parts = []
        for _ in range(3):
            part = m.astype(jnp.bfloat16).astype(jnp.float32)
            m = m - part
            parts.append(part)
        spread[slot] = jnp.concatenate(parts, axis=1)

    def spread_row(slot, x):
        left = (keep * spread[slot, pl.ds(x, 1), :]).astype(jnp.bfloat16)
        wide = jnp.dot(left, ones, preferred_element_type=jnp.float32)
        M[slot, x] = wide.reshape(nq, 2 * nf, lanes)

    split(0, diag_ref[0])
    split(1, cross_ref[...])
    split(2, diag_ref[1])
    for x in range(nx):
        for slot in range(3):
            spread_row(slot, x)

    def laplace(src, ex, ey):
        u = [[src[4 * ex + a, 2 * ey + p] for p in range(2)] for a in range(4)]
        fx = [[None] * 2 for _ in range(4)]
        fy = [[None] * 2 for _ in range(4)]
        for a in range(4):
            mix = [u[a][0], swap(u[a][0]), u[a][1], swap(u[a][1])]
            for p in range(2):
                at = (4 * ex + a, 2 * ey + p)
                gx = dot4(D[a], [u[b][p] for b in range(4)])
                gy = dot4(D_half[p], mix)
                m0, mc, m1 = M[(0,) + at], M[(1,) + at], M[(2,) + at]
                fx[a][p] = m0 * gx + mc * gy
                fy[a][p] = mc * gx + m1 * gy
        for a in range(4):
            mix = [fy[a][0], swap(fy[a][0]), fy[a][1], swap(fy[a][1])]
            for p in range(2):
                W[4 * ex + a, 2 * ey + p] = dot4(
                    minus_t[a], [fx[b][p] for b in range(4)]
                ) + dot4(minus_half[p], mix)

    def rows_sum(x, q):
        if x % 4 == 0 and x > 0:
            return W[x, q] + W[x - 1, q]
        if x % 4 == 3 and x < nx - 1:
            return W[x, q] + W[x + 1, q]
        return W[x, q]

    def assemble_row(x):
        line = [rows_sum(x, q) for q in range(nq)]
        for ey in range(1, nby):
            v, w = line[2 * ey - 1], line[2 * ey]
            line[2 * ey - 1], line[2 * ey] = v + high * swap(w), w + low * swap(v)
        for q in range(nq):
            T[x, q] = line[q]
            if x % 4 == 3 and x < nx - 1:
                T[x + 1, q] = line[q]

    def send(phase, k, src, dst):
        copy = pltpu.make_async_remote_copy(
            src_ref=src, dst_ref=dst,
            send_sem=send_sem.at[phase, k], recv_sem=recv_sem.at[phase, opposite[k]],
            device_id=peers[k], device_id_type=MESH,
        )
        copy.start()
        return copy

    def phase_sends(phase, src, sC, rR, rC, rK, ready):
        copies = [None] * 8
        for ex in order[:2]:
            ready(ex)
            for ey in range(nby):
                laplace(src, ex, ey)
        for x in (0, nx - 1):
            assemble_row(x)
        if phase == 0:
            pl.semaphore_wait(barrier, len(peers))
        for s in range(2):
            for t in range(2):
                k = 4 + 2 * s + t
                copies[k] = send(
                    phase, k, W.at[s * (nx - 1), t * (nq - 1)], rK.at[3 - 2 * s - t]
                )
        for s in range(2):
            copies[s] = send(phase, s, T.at[s * (nx - 1)], rR.at[1 - s])
        if phase == 0:
            for k in range(8):
                masses.append(
                    pltpu.make_async_remote_copy(
                        src_ref=mass_ref, dst_ref=rM.at[opposite[k]],
                        send_sem=mass_send.at[k], recv_sem=mass_recv.at[opposite[k]],
                        device_id=peers[k], device_id_type=MESH,
                    )
                )
                masses[-1].start()
        for ex in order[2:]:
            ready(ex)
            for ey in range(nby):
                laplace(src, ex, ey)
        for k in range(nx // 2):
            a, b = rows_sum(2 * k, 0), rows_sum(2 * k + 1, 0)
            sC[0, k] = jnp.where(is_low, a, swap(b))
            a, b = rows_sum(2 * k, nq - 1), rows_sum(2 * k + 1, nq - 1)
            sC[1, k] = jnp.where(is_low, swap(a), b)
        for t in range(2):
            copies[2 + t] = send(phase, 2 + t, sC.at[t], rC.at[1 - t])
        for x in range(1, nx - 1):
            if x % 4 != 0:
                assemble_row(x)
        return copies

    def finished(x, rR, rC, rK):
        line = [T[x, q] for q in range(nq)]
        if x in (0, nx - 1):
            s = 0 if x == 0 else 1
            line = [v + rR[s, q] for q, v in enumerate(line)]
            line[0] = line[0] + low * swap(rK[2 * s])
            line[-1] = line[-1] + high * swap(rK[2 * s + 1])
        before, after = rC[0, x // 2], rC[1, x // 2]
        if x % 2 == 0:
            after = swap(after)
        else:
            before = swap(before)
        line[0] = line[0] + low * before
        line[-1] = line[-1] + high * after
        return line

    masses = []
    first_copies = phase_sends(0, raw, sC1, rR1, rC1, rK1, lambda ex: loads[ex].wait())

    for copy in masses:
        copy.wait_recv()
    x_at = lax.broadcasted_iota(jnp.int32, (nx, ny), 0)
    y_at = lax.broadcasted_iota(jnp.int32, (nx, ny), 1)
    x_low, x_high = (x_at & 3) == 0, (x_at & 3) == 3
    y_low, y_high = (y_at & 3) == 0, (y_at & 3) == 3

    def mass_rows(own, prev, nxt):
        down = jnp.concatenate([prev[nx - 1:], own[: nx - 1]], axis=0)
        up = jnp.concatenate([own[1:], nxt[:1]], axis=0)
        return own + jnp.where(x_low, down, 0.0) + jnp.where(x_high, up, 0.0)

    here = mass_rows(mass_ref[...], rM[0], rM[1])
    left = mass_rows(rM[2], rM[4], rM[6])
    right = mass_rows(rM[3], rM[5], rM[7])
    back = jnp.concatenate([left[:, ny - 1:], here[:, : ny - 1]], axis=1)
    ahead = jnp.concatenate([here[:, 1:], right[:, :1]], axis=1)
    mass_sum = here + jnp.where(y_low, back, 0.0) + jnp.where(y_high, ahead, 0.0)
    split(3, 1.0 / mass_sum)
    for x in range(nx):
        spread_row(3, x)

    for copy in first_copies:
        copy.wait_recv()
    for x in range(nx):
        line = finished(x, rR1, rC1, rK1)
        for q in range(nq):
            U[x, q] = line[q] * M[3, x, q]
    for copy in first_copies:
        copy.wait_send()

    second_copies = phase_sends(1, U, sC2, rR2, rC2, rK2, lambda ex: None)
    for copy in second_copies:
        copy.wait_recv()
    for x in range(nx):
        line = finished(x, rR2, rC2, rK2)
        for q in range(nq):
            out_ref[x, q] = line[q] * M[3, x, q]
    for copy in second_copies + masses:
        copy.wait_send()


def solution(mesh):
    faces, cols = mesh.shape["face"], mesh.shape["col"]

    def shards(fields, metric_diag, metric_cross, point_mass):
        nf, nx, ny, lanes = fields.shape
        nbx, nby = nx // 4, ny // 4
        f32 = jnp.float32
        tiles = (nx, ny // 2, 2 * nf, lanes)

        def vmem(*shape):
            return pltpu.VMEM(shape, f32)

        def landing():
            return [
                vmem(2, nx // 2, 2 * nf, lanes),
                vmem(2, ny // 2, 2 * nf, lanes),
                vmem(2, nx // 2, 2 * nf, lanes),
                vmem(4, 2 * nf, lanes),
            ]

        out = pl.pallas_call(
            functools.partial(kernel, faces, cols, nf, nbx, nby),
            out_shape=jax.ShapeDtypeStruct(tiles, f32),
            in_specs=[pl.BlockSpec(memory_space=pl.ANY)]
            + [pl.BlockSpec(memory_space=pltpu.VMEM)] * 3,
            out_specs=pl.BlockSpec(memory_space=pltpu.VMEM),
            scratch_shapes=[
                vmem(*tiles),
                vmem(*tiles),
                vmem(4, *tiles),
                vmem(*tiles),
                vmem(*tiles),
                vmem(4, nx, 3 * ny),
                vmem(8, nx, ny),
                *landing(), *landing(),
                pltpu.SemaphoreType.DMA((nbx,)),
                pltpu.SemaphoreType.DMA((8,)),
                pltpu.SemaphoreType.DMA((8,)),
                pltpu.SemaphoreType.DMA((2, 8)),
                pltpu.SemaphoreType.DMA((2, 8)),
            ],
            compiler_params=pltpu.CompilerParams(
                collective_id=0, has_side_effects=True, vmem_limit_bytes=32 * 1024 * 1024
            ),
        )(
            fields.transpose(1, 2, 0, 3).reshape(tiles),
            metric_diag, metric_cross, point_mass,
        )
        return out.reshape(nx, ny, nf, lanes).transpose(2, 0, 1, 3)

    return jax.shard_map(
        shards,
        mesh=mesh,
        in_specs=(
            P(None, "face", "col", None),
            P(None, "face", "col"),
            P("face", "col"),
            P("face", "col"),
        ),
        out_specs=P(None, "face", "col", None),
        check_vma=False,
    )
```

profile of v0, /device:TPU:0, one launch (start us, length us, event | category | flops | bytes accessed | tf_op | source)
XLA Modules:
  0.0 21.8 jit_solution(15306638310891589113)
XLA Ops:
  0.0 0.0 copy-start.1
  0.0 0.0 copy-start.2
  0.0 0.8 %copy.5.diag_ref = f32[2,20,20]{2,1,0:T(8,128)S(1)} copy(f32[2,20,20]{2,0,1:T(2,128)} %param.5) | data formatting | bytes 6400 | tf_op args[1]
  0.8 0.0 copy-done.1
  0.8 0.0 copy-done.2
  0.8 0.0 copy-start
  0.8 1.1 %copy-done = f32[4,20,20,128]{3,0,2,1:T(4,128)S(1)} copy-done((f32[4,20,20,128]{3,0,2,1:T(4,128)S(1)}, f32[4,20,20,128]{3,0,2,1:T(4,128)}, u32[]{:S(2)}) %copy-start) | copy-done | bytes 819224
  1.9 19.0 %shard_map.46 = f32[20,10,8,128]{3,2,1,0:T(8,128)S(1)} custom-call(f32[20,10,8,128]{3,2,1,0:T(8,128)S(1)} %bitcast.7, f32[2,20,20]{2,1,0:T(8,128)S(1)} %copy.5.diag_ref, f32[20,20]{1,0:T(8,128)S(1)} %copy-done.1, f32[20,20]{1,0:T(8,128)S(1)} %copy-done.2), custom_call_target="tpu_custom_call" | custom-call | tf_op jit(solution)/shard_map/pallas_call | solution.py:289
  20.9 0.9 %copy.7 = f32[4,20,20,128]{3,0,2,1:T(4,128)} copy(f32[4,20,20,128]{3,0,2,1:T(4,128)S(1)} %bitcast.6) | data formatting | bytes 1638400
Async XLA Ops:
  0.0 0.8 %copy-start.1 = (f32[20,20]{1,0:T(8,128)S(1)}, f32[20,20]{1,0:T(8,128)}, u32[]{:S(2)}) copy-start(f32[20,20]{1,0:T(8,128)} %cross_ref.1) | copy-start | bytes 4804
  0.0 0.8 %copy-start.2 = (f32[20,20]{1,0:T(8,128)S(1)}, f32[20,20]{1,0:T(8,128)}, u32[]{:S(2)}) copy-start(f32[20,20]{1,0:T(8,128)} %mass_ref.1) | copy-start | bytes 4804
  0.8 1.1 %copy-start = (f32[4,20,20,128]{3,0,2,1:T(4,128)S(1)}, f32[4,20,20,128]{3,0,2,1:T(4,128)}, u32[]{:S(2)}) copy-start(f32[4,20,20,128]{3,0,2,1:T(4,128)} %param.4) | copy-start | bytes 2457604
where the time goes:
time: 22 us; the launch traced here: 21.8 us
  Pallas kernels  19 us (86%)
  local copies, waits for them, and re-layouts  2.79 us (13%)
    pallas_call x1, Pallas kernels, shards(): pl.pallas_call(functools.partial(kernel, faces, cols, nf, nbx, nby), out_...  19 us
    unnamed x8, local copies, waits for them, and re-layouts  2.79 us

commit v1 on v0

--- a/solution.py
+++ b/solution.py
@@ -39,10 +39,10 @@
 
 def kernel(
     faces, cols, nf, nbx, nby,
-    fields_hbm, diag_ref, cross_ref, mass_ref, out_ref,
-    raw, U, M, W, T, spread, rM,
+    fields_hbm, diag_hbm, cross_hbm, mass_hbm, out_ref,
+    diag_ref, cross_ref, mass_ref, raw, U, M, W, T, spread, rM,
     sC1, rR1, rC1, rK1, sC2, rR2, rC2, rK2,
-    load_sem, mass_send, mass_recv, send_sem, recv_sem,
+    small_sem, load_sem, mass_send, mass_recv, send_sem, recv_sem,
 ):
     face, col = lax.axis_index("face"), lax.axis_index("col")
     fside = (lax.rem(face + faces - 1, faces), lax.rem(face + 1, faces))
@@ -53,6 +53,10 @@
 
     nx, ny, nq = 4 * nbx, 4 * nby, 2 * nby
     lanes = raw.shape[-1]
+    barrier = pltpu.get_barrier_semaphore()
+    for peer in peers:
+        pl.semaphore_signal(barrier, inc=1, device_id=peer, device_id_type=MESH)
+
     order = [0, nbx - 1] + list(range(1, nbx - 1))
     loads = {
         ex: pltpu.make_async_copy(
@@ -60,11 +64,18 @@
         )
         for ex in order
     }
+    small = [
+        pltpu.make_async_copy(src, dst, small_sem.at[k])
+        for k, (src, dst) in enumerate(
+            ((diag_hbm, diag_ref), (cross_hbm, cross_ref), (mass_hbm, mass_ref))
+        )
+    ]
+    for copy in small:
+        copy.start()
     for ex in order:
         loads[ex].start()
-    barrier = pltpu.get_barrier_semaphore()
-    for peer in peers:
-        pl.semaphore_signal(barrier, inc=1, device_id=peer, device_id_type=MESH)
+    for copy in small:
+        copy.wait()
 
     D = derivative_table()
     sub = lax.broadcasted_iota(jnp.int32, (2 * nf, lanes), 0)
@@ -108,9 +119,9 @@
         wide = jnp.dot(left, ones, preferred_element_type=jnp.float32)
         M[slot, x] = wide.reshape(nq, 2 * nf, lanes)
 
-    split(0, diag_ref[0])
+    split(0, diag_ref[:, 0, :])
     split(1, cross_ref[...])
-    split(2, diag_ref[1])
+    split(2, diag_ref[:, 1, :])
     for x in range(nx):
         for slot in range(3):
             spread_row(slot, x)
@@ -289,10 +300,12 @@
         out = pl.pallas_call(
             functools.partial(kernel, faces, cols, nf, nbx, nby),
             out_shape=jax.ShapeDtypeStruct(tiles, f32),
-            in_specs=[pl.BlockSpec(memory_space=pl.ANY)]
-            + [pl.BlockSpec(memory_space=pltpu.VMEM)] * 3,
+            in_specs=[pl.BlockSpec(memory_space=pltpu.HBM)] * 4,
             out_specs=pl.BlockSpec(memory_space=pltpu.VMEM),
             scratch_shapes=[
+                vmem(nx, 2, ny),
+                vmem(nx, ny),
+                vmem(nx, ny),
                 vmem(*tiles),
                 vmem(*tiles),
                 vmem(4, *tiles),
@@ -301,6 +314,7 @@
                 vmem(4, nx, 3 * ny),
                 vmem(8, nx, ny),
                 *landing(), *landing(),
+                pltpu.SemaphoreType.DMA((3,)),
                 pltpu.SemaphoreType.DMA((nbx,)),
                 pltpu.SemaphoreType.DMA((8,)),
                 pltpu.SemaphoreType.DMA((8,)),
@@ -308,11 +322,11 @@
                 pltpu.SemaphoreType.DMA((2, 8)),
             ],
             compiler_params=pltpu.CompilerParams(
-                collective_id=0, has_side_effects=True, vmem_limit_bytes=32 * 1024 * 1024
+                collective_id=0, has_side_effects=True, vmem_limit_bytes=45000000
             ),
         )(
             fields.transpose(1, 2, 0, 3).reshape(tiles),
-            metric_diag, metric_cross, point_mass,
+            metric_diag.transpose(1, 0, 2), metric_cross, point_mass,
         )
         return out.reshape(nx, ny, nf, lanes).transpose(2, 0, 1, 3)
 

time: 22 us -> 22.4 us (1.018)
  local copies, waits for them, and re-layouts: 2.79 us -> 4.18 us
  Pallas kernels: 19 us -> 17.9 us
    unnamed x8 -> x9, local copies, waits for them, and re-layouts: 2.79 us -> 4.18 us
    pallas_call x1, Pallas kernels: 19 us -> 17.9 us  [shards(): pl.pallas_call(functools.partial(kernel, faces, cols, nf, nbx, nby), out_...]
where the time goes in v1:
time: 22.4 us; the launch traced here: 22.1 us
  Pallas kernels  17.9 us (80%)
  local copies, waits for them, and re-layouts  4.18 us (19%)
    pallas_call x1, Pallas kernels, shards(): pl.pallas_call(functools.partial(kernel, faces, cols, nf, nbx, nby), out_...  17.9 us
    unnamed x9, local copies, waits for them, and re-layouts  4.18 us

profile of v1, /device:TPU:0, one launch (start us, length us, event | category | flops | bytes accessed | tf_op | source)
XLA Modules:
  0.0 22.1 jit_solution(17990369863200088422)
XLA Ops:
  0.0 0.0 copy-start
  0.0 1.1 %copy-done = f32[4,20,20,128]{3,0,2,1:T(4,128)S(1)} copy-done((f32[4,20,20,128]{3,0,2,1:T(4,128)S(1)}, f32[4,20,20,128]{3,0,2,1:T(4,128)}, u32[]{:S(2)}) %copy-start) | copy-done | bytes 819224
  1.1 0.0 copy-start.1
  1.1 0.7 %copy-done.1 = f32[2,20,20]{2,0,1:T(2,128)S(1)} copy-done((f32[2,20,20]{2,0,1:T(2,128)S(1)}, f32[2,20,20]{2,0,1:T(2,128)}, u32[]{:S(2)}) %copy-start.1) | copy-done | bytes 3224
  1.9 0.0 copy-start.2
  1.9 0.7 %copy-done.2 = f32[20,20]{1,0:T(8,128)S(1)} copy-done((f32[20,20]{1,0:T(8,128)S(1)}, f32[20,20]{1,0:T(8,128)}, u32[]{:S(2)}) %copy-start.2) | copy-done | bytes 1624
  2.6 0.0 copy-start.3
  2.6 0.7 %copy-done.3 = f32[20,20]{1,0:T(8,128)S(1)} copy-done((f32[20,20]{1,0:T(8,128)S(1)}, f32[20,20]{1,0:T(8,128)}, u32[]{:S(2)}) %copy-start.3) | copy-done | bytes 1624
  3.3 17.9 %shard_map.46 = f32[20,10,8,128]{3,2,1,0:T(8,128)S(1)} custom-call(f32[20,10,8,128]{3,2,1,0:T(8,128)S(1)} %bitcast.8, f32[20,2,20]{2,1,0:T(2,128)S(1)} %bitcast.9, f32[20,20]{1,0:T(8,128)S(1)} %copy-done.2, f32[20,20]{1,0:T(8,128)S(1)} %copy-done.3), custom_call_target="tpu_custom_call" | custom-call | tf_op jit(solution)/shard_map/pallas_call | solution.py:300
  21.2 0.9 %copy.6 = f32[4,20,20,128]{3,0,2,1:T(4,128)} copy(f32[4,20,20,128]{3,0,2,1:T(4,128)S(1)} %bitcast.7) | data formatting | bytes 1638400
Async XLA Ops:
  0.0 1.1 %copy-start = (f32[4,20,20,128]{3,0,2,1:T(4,128)S(1)}, f32[4,20,20,128]{3,0,2,1:T(4,128)}, u32[]{:S(2)}) copy-start(f32[4,20,20,128]{3,0,2,1:T(4,128)} %param.4) | copy-start | bytes 2457604
  1.1 0.7 %copy-start.1 = (f32[2,20,20]{2,0,1:T(2,128)S(1)}, f32[2,20,20]{2,0,1:T(2,128)}, u32[]{:S(2)}) copy-start(f32[2,20,20]{2,0,1:T(2,128)} %param.5) | copy-start | bytes 9604
  1.9 0.7 %copy-start.2 = (f32[20,20]{1,0:T(8,128)S(1)}, f32[20,20]{1,0:T(8,128)}, u32[]{:S(2)}) copy-start(f32[20,20]{1,0:T(8,128)} %cross_hbm.1) | copy-start | bytes 4804
  2.6 0.7 %copy-start.3 = (f32[20,20]{1,0:T(8,128)S(1)}, f32[20,20]{1,0:T(8,128)}, u32[]{:S(2)}) copy-start(f32[20,20]{1,0:T(8,128)} %mass_hbm.1) | copy-start | bytes 4804

commit v2 on v1

--- a/solution.py
+++ b/solution.py
@@ -322,12 +322,15 @@
                 pltpu.SemaphoreType.DMA((2, 8)),
             ],
             compiler_params=pltpu.CompilerParams(
-                collective_id=0, has_side_effects=True, vmem_limit_bytes=45000000
+                collective_id=0, has_side_effects=True, vmem_limit_bytes=32 * 1024 * 1024
             ),
-        )(
-            fields.transpose(1, 2, 0, 3).reshape(tiles),
-            metric_diag.transpose(1, 0, 2), metric_cross, point_mass,
-        )
+        )(*[
+            pltpu.with_memory_space_constraint(v, pltpu.HBM)
+            for v in (
+                fields.transpose(1, 2, 0, 3).reshape(tiles),
+                metric_diag.transpose(1, 0, 2), metric_cross, point_mass,
+            )
+        ])
         return out.reshape(nx, ny, nf, lanes).transpose(2, 0, 1, 3)
 
     return jax.shard_map(

time: 22.4 us -> 19 us (0.85)
  local copies, waits for them, and re-layouts: 4.18 us -> 0.89 us
    unnamed x9 -> x1, local copies, waits for them, and re-layouts: 4.18 us -> 0.89 us
where the time goes in v2:
time: 19 us; the launch traced here: 18.8 us
  Pallas kernels  17.9 us (94%)
  local copies, waits for them, and re-layouts  0.89 us (5%)
    pallas_call x1, Pallas kernels, shards(): pl.pallas_call(functools.partial(kernel, faces, cols, nf, nbx, nby), out_...  17.9 us
    unnamed x1, local copies, waits for them, and re-layouts  0.89 us

profile of v2, /device:TPU:0, one launch (start us, length us, event | category | flops | bytes accessed | tf_op | source)
XLA Modules:
  0.0 18.8 jit_solution(7572326291831930336)
XLA Ops:
  0.0 17.9 %shard_map.46 = f32[20,10,8,128]{3,2,1,0:T(8,128)S(1)} custom-call(f32[20,10,8,128]{3,2,1,0:T(8,128)} %bitcast.8, f32[20,2,20]{2,1,0:T(2,128)} %bitcast.9, f32[20,20]{1,0:T(8,128)} %cross_hbm.1, f32[20,20]{1,0:T(8,128)} %mass_hbm.1), custom_call_target="tpu_custom_call" | custom-call | tf_op jit(solution)/shard_map/pallas_call | solution.py:300
  18.0 0.9 %copy.6 = f32[4,20,20,128]{3,0,2,1:T(4,128)} copy(f32[4,20,20,128]{3,0,2,1:T(4,128)S(1)} %bitcast.7) | data formatting | bytes 1638400

commit v3 on v2

v3 whole, which is shorter than its diff:
```python
import functools

import jax
import jax.numpy as jnp
import numpy as np
from jax import lax
from jax.experimental import pallas as pl
from jax.experimental.pallas import tpu as pltpu
from jax.sharding import PartitionSpec as P

MESH = pl.DeviceIdType.MESH


def derivative_table():
    small = 1.0 / np.sqrt(5.0)
    nodes = np.array([-1.0, -small, small, 1.0])
    count = nodes.shape[0]
    weights = np.array(
        [np.prod([nodes[a] - nodes[k] for k in range(count) if k != a]) for a in range(count)]
    )
    table = np.zeros((count, count))
    for a in range(count):
        for b in range(count):
            if a == b:
                table[a, b] = np.sum([1.0 / (nodes[a] - nodes[k]) for k in range(count) if k != a])
            else:
                table[a, b] = weights[a] / weights[b] / (nodes[a] - nodes[b])
    return [[float(np.float32(v)) for v in row] for row in table]


def add(a, b):
    if a is None or b is None:
        return b if a is None else a
    return a + b


def mul(a, b):
    return None if b is None else a * b


def combine(coefs, terms):
    total = None
    for c, t in zip(coefs, terms):
        if isinstance(c, float) and c == 0.0:
            continue
        total = add(total, mul(c, t))
    return total


def kernel(
    faces, cols, nf, nbx, nby,
    fields_hbm, diag_hbm, cross_hbm, mass_hbm, out_ref,
    diag_ref, cross_ref, mass_ref, raw, U, W, T, side, met, B, Br, Bc, Bd,
    sRA, sRB, sCA, sCB, sD, rRA, rRB, rCA, rCB, rD, rMr, rMc, rMd,
    small_sem, load_sem, send_sem, recv_sem, late,
):
    face, col = lax.axis_index("face"), lax.axis_index("col")
    fside = (lax.rem(face + faces - 1, faces), lax.rem(face + 1, faces))
    cside = (lax.rem(col + cols - 1, cols), lax.rem(col + 1, cols))
    peers = [(fside[0], col), (fside[1], col), (face, cside[0]), (face, cside[1])]
    peers += [(fside[s], cside[t]) for s in range(2) for t in range(2)]
    opposite = [1, 0, 3, 2, 7, 6, 5, 4]
    before, after = [0, 4, 5], [1, 6, 7]

    barrier = pltpu.get_barrier_semaphore()
    for k in (2, 3, *before):
        pl.semaphore_signal(barrier, inc=1, device_id=peers[k], device_id_type=MESH)

    @pl.when(face != faces - 1)
    def _():
        for k in after:
            pl.semaphore_signal(barrier, inc=1, device_id=peers[k], device_id_type=MESH)

    nx, ny, nq = 4 * nbx, 4 * nby, 2 * nby
    lanes = raw.shape[-1]
    tile = (2 * nf, lanes)
    order = [nbx - 1, nbx - 2] + list(range(nbx - 2))
    small = [
        pltpu.make_async_copy(src, dst, small_sem.at[k])
        for k, (src, dst) in enumerate(
            ((diag_hbm, diag_ref), (cross_hbm, cross_ref), (mass_hbm, mass_ref))
        )
    ]
    loads = {
        ex: pltpu.make_async_copy(
            fields_hbm.at[pl.ds(4 * ex, 4)], raw.at[pl.ds(4 * ex, 4)], load_sem.at[ex]
        )
        for ex in order
    }
    for copy in small:
        copy.start()
    for ex in order:
        loads[ex].start()

    D = derivative_table()
    is_low = lax.broadcasted_iota(jnp.int32, tile, 0) < nf
    lane = lax.broadcasted_iota(jnp.int32, tile, 1)
    low = jnp.where(is_low, 1.0, 0.0)
    high = 1.0 - low

    def swap(v):
        return pltpu.roll(v, nf, 0)

    def halves(table):
        return [
            [
                jnp.where(is_low, table[2 * p][2 * q + k], table[2 * p + 1][2 * q + 1 - k])
                for q in range(2) for k in range(2)
            ]
            for p in range(2)
        ]

    minus_t = [[-D[b][a] for b in range(4)] for a in range(4)]
    D_half, minus_half = halves(D), halves(minus_t)

    def mixed(v, w):
        return [v, None if v is None else swap(v), w, None if w is None else swap(w)]

    def laplace(u, m):
        @functools.cache
        def mix(a):
            return mixed(*u[a])

        @functools.cache
        def flux(a, p):
            gx = combine(D[a], [u[b][p] for b in range(4)])
            gy = combine(D_half[p], mix(a))
            return gx, gy

        @functools.cache
        def fx(a, p):
            gx, gy = flux(a, p)
            return add(
                None if gx is None else m(0, a, p) * gx, None if gy is None else m(1, a, p) * gy
            )

        @functools.cache
        def mix_fy(a):
            parts = []
            for p in range(2):
                gx, gy = flux(a, p)
                parts.append(add(
                    None if gx is None else m(1, a, p) * gx, None if gy is None else m(2, a, p) * gy
                ))
            return mixed(*parts)

        def w(a, p):
            return add(
                combine(minus_t[a], [fx(b, p) for b in range(4)]), combine(minus_half[p], mix_fy(a))
            )

        return w

    def wide(row):
        return jnp.broadcast_to(row, tile)

    def in_all_lanes(v, y):
        return jnp.broadcast_to(v[:, y:y + 1], tile)

    def tile_of(column, p):
        return jnp.where(is_low, wide(column(2 * p)), wide(column(2 * p + 1)))

    def metrics(ref, *at):
        return functools.cache(
            lambda slot, a, p: tile_of(lambda j: ref[(*at, j, pl.ds(4 * slot + a, 1))], p)
        )

    def own_metrics(ex, ey):
        return functools.cache(lambda slot, a, p: tile_of(
            lambda j: B[ex, 4 * ey + j, 4 * slot + a:4 * slot + a + 1, :], p
        ))

    def inverse_mass(x, q):
        return own_metrics(x // 4, q // 2)(3, x % 4, q % 2)

    def send(phase, k, src, dst, start=True):
        copy = pltpu.make_async_remote_copy(
            src_ref=src, dst_ref=dst,
            send_sem=send_sem.at[phase, k], recv_sem=recv_sem.at[phase, opposite[k]],
            device_id=peers[k], device_id_type=MESH,
        )
        if start:
            copy.start()
        copies[phase, k] = copy
        return copy

    def arrived(phase, k):
        copies[phase, opposite[k]].wait_recv()

    held = []

    def send_back(*those):
        made = [send(*one, start=False) for one in those]
        held.extend(made)

        @pl.when(face != 0)
        def _():
            for copy in made:
                copy.start()

    copies = {}

    for copy in small:
        copy.wait()
    mass = mass_ref[...]
    x_at = lax.broadcasted_iota(jnp.int32, (nx, ny), 0)
    y_at = lax.broadcasted_iota(jnp.int32, (nx, ny), 1)
    zero_row, zero_col = jnp.zeros((1, ny), jnp.float32), jnp.zeros((nx, 1), jnp.float32)
    down = jnp.concatenate([zero_row, mass[: nx - 1]], axis=0)
    up = jnp.concatenate([mass[1:], zero_row], axis=0)
    mass = mass + jnp.where((x_at & 3) == 0, down, 0.0) + jnp.where((x_at & 3) == 3, up, 0.0)
    back = jnp.concatenate([zero_col, mass[:, : ny - 1]], axis=1)
    ahead = jnp.concatenate([mass[:, 1:], zero_col], axis=1)
    mass = mass + jnp.where((y_at & 3) == 0, back, 0.0) + jnp.where((y_at & 3) == 3, ahead, 0.0)
    cross = cross_ref[...]
    for slot, v in enumerate((diag_ref[:, 0, :], cross, diag_ref[:, 1, :], mass)):
        for ex in range(nbx):
            met[ex, 4 * slot:4 * slot + 4, :ny] = v[4 * ex:4 * ex + 4]

    pl.semaphore_wait(barrier, jnp.where(face == 0, 5, 8))

    @pl.when(face == faces - 1)
    def _():
        for k in after:
            pl.semaphore_signal(late, inc=1, device_id=peers[k], device_id_type=MESH)

    send(0, 1, met.at[nbx - 1], rMr.at[0])
    for t in range(2):
        send(0, 6 + t, met.at[nbx - 1], rMd.at[1 - t])
    for t in range(2):
        send(0, 2 + t, met, rMc.at[1 - t])
    send_back((0, 0, met.at[0], rMr.at[1]), (0, 4, met.at[0], rMd.at[3]), (0, 5, met.at[0], rMd.at[2]))

    sub = lax.broadcasted_iota(jnp.int32, tile, 0)
    halves_of = [pl.ds(8 * i, 8) for i in range(2)]

    def inverted(ex, mass_of=lambda v: v):
        v = met[ex, halves_of[1], :]
        return jnp.where(sub < 4, v, 1.0 / mass_of(v))

    for ex in order:
        v, w = met[ex, halves_of[0], :], inverted(ex)
        for y in range(ny):
            B[ex, y, halves_of[0], :] = in_all_lanes(v, y)
            B[ex, y, halves_of[1], :] = in_all_lanes(w, y)

    def lift(ref, at, to, ys):
        for half in halves_of:
            v = ref[(*at, half)]
            for i, y in enumerate(ys):
                to[(*at, i, half)] = in_all_lanes(v, y)

    def rows_sum(src, x, *at):
        if x % 4 == 0 and x > 0:
            return src(x, *at) + src(x - 1, *at)
        if x % 4 == 3 and x < nx - 1:
            return src(x, *at) + src(x + 1, *at)
        return src(x, *at)

    def across(line):
        for ey in range(1, nby):
            v, w = line[2 * ey - 1], line[2 * ey]
            line[2 * ey - 1], line[2 * ey] = v + high * swap(w), w + low * swap(v)
        return line

    def in_W(x, q):
        return W[x, q]

    def first_laplacian(ex):
        loads[ex].wait()
        for ey in range(nby):
            w = laplace(
                [[raw[4 * ex + a, 2 * ey + p] for p in range(2)] for a in range(4)],
                own_metrics(ex, ey),
            )
            for a in range(4):
                for p in range(2):
                    W[4 * ex + a, 2 * ey + p] = w(a, p)

    def first_rows(xs):
        for x in xs:
            if x % 4 == 0 and x > 0:
                continue
            line = across([rows_sum(in_W, x, q) for q in range(nq)])
            for q in range(nq):
                T[x, q] = line[q]
                if x % 4 == 3 and x < nx - 1:
                    T[x + 1, q] = line[q]

    def inner_first(xs):
        for x in xs:
            for q in range(nq):
                v = T[x, q] * inverse_mass(x, q)
                U[x, q] = high * v if q == 0 else low * v if q == nq - 1 else v

    def known(ex, ey):
        return [
            [None if x in (0, nx - 1) else U[x, 2 * ey + p] for p in range(2)]
            for x in range(4 * ex, 4 * ex + 4)
        ]

    def known_parts(ex):
        edge = {0: (0, 0), nbx - 1: (1, 3)}.get(ex)
        line = [None] * nq
        for ey in range(nby):
            if edge is None and 0 < ey < nby - 1:
                continue
            w = laplace(known(ex, ey), own_metrics(ex, ey))
            if edge:
                line[2 * ey], line[2 * ey + 1] = w(edge[1], 0), w(edge[1], 1)
            for t, e in ((0, 0), (1, nby - 1)):
                if ey == e:
                    for a in range(4):
                        side[t, 4 * ex + a] = w(a, t)
        if edge:
            line = across(line)
            for q in range(nq):
                sRB[edge[0], q] = line[q]

    def stage_row(s):
        xe, near = s * (nx - 1), (nx - 4 if s else 1)
        for q in range(nq):
            sRA[s, q] = T[xe, q]
        for i in range(3):
            sRA[s, nq + i] = jnp.where(is_low, T[near + i, 0], T[near + i, nq - 1])

    def stage_corner(s, t):
        xe, near, q = s * (nx - 1), (nx - 4 if s else 1), t * (nq - 1)
        for p in range(2):
            sD[2 * s + t, p] = T[xe, t * (nq - 2) + p]
        halves = [T[near + i, q] for i in range(3)] + [sRB[s, q]]
        for i in range(2):
            v, w = halves[2 * i], halves[2 * i + 1]
            sD[2 * s + t, 2 + i] = (
                jnp.where(is_low, swap(v), w) if t else jnp.where(is_low, v, swap(w))
            )

    def pack_column(t, v, w):
        return jnp.where(is_low, swap(v), w) if t else jnp.where(is_low, v, swap(w))

    for ex in order[:2]:
        first_laplacian(ex)
    first_rows(range(nx - 5, nx))
    stage_row(1)
    send(1, 1, sRA.at[1], rRA.at[0])
    inner_first(range(nx - 4, nx - 1))
    known_parts(nbx - 1)
    for t in range(2):
        stage_corner(1, t)
        send(1, 6 + t, sD.at[2 + t], rD.at[1 - t])
    send(2, 1, sRB.at[1], rRB.at[0])

    for ex in order[2:]:
        first_laplacian(ex)
    first_rows(range(nx - 5))
    for t in range(2):
        q = t * (nq - 1)
        for k in range(nx // 2):
            sCA[t, k] = pack_column(t, T[2 * k, q], T[2 * k + 1, q])
        for s in range(2):
            for p in range(2):
                sCA[t, nx // 2 + 2 * s + p] = T[s * (nx - 1), t * (nq - 2) + p]
        send(1, 2 + t, sCA.at[t], rCA.at[1 - t])
    stage_row(0)
    send_back((1, 0, sRA.at[0], rRA.at[1]))
    inner_first(range(1, nx - 4))
    for ex in range(nbx - 1):
        known_parts(ex)
    for t in range(2):
        stage_corner(0, t)
    send_back(
        (1, 4, sD.at[0], rD.at[3]), (1, 5, sD.at[1], rD.at[2]), (2, 0, sRB.at[0], rRB.at[1])
    )
    for t in range(2):
        def in_side(x, t=t):
            return side[t, x]

        for k in range(nx // 2):
            sCB[t, k] = pack_column(t, rows_sum(in_side, 2 * k), rows_sum(in_side, 2 * k + 1))
        send(2, 2 + t, sCB.at[t], rCB.at[1 - t])

    @pl.when(face == 0)
    def _():
        pl.semaphore_wait(late, 3)
        for copy in held:
            copy.start()

    def mass_row(ref, *at):
        return wide(ref[(*at[:-1], pl.ds(12 + at[-1], 1))])

    def with_sides(mid, left, right):
        return (
            mid
            + jnp.where(lane == 0, pltpu.roll(left, lanes - (ny - 1), 1), 0.0)
            + jnp.where(lane == ny - 1, pltpu.roll(right, ny - 1, 1), 0.0)
        )

    def column_part(ref, t, x):
        v = ref[t, x // 2]
        if x % 2 != t:
            v = swap(v)
        return (high if t else low) * v

    def second_elements(ex, eys):
        for ey in eys:
            w = laplace(
                [[U[4 * ex + a, 2 * ey + p] for p in range(2)] for a in range(4)],
                own_metrics(ex, ey),
            )
            for a in range(4):
                for p in range(2):
                    W[4 * ex + a, 2 * ey + p] = w(a, p)

    def side_elements(t, ex, row=None, ext=None):
        u = []
        for a in range(4):
            v = swap(U[4 * ex + a, t * (nq - 1)])
            u.append([low * v, None] if t else [None, high * v])
        if row is not None:
            u[row] = ext
        w = laplace(u, metrics(Bc, t, ex))
        for a in range(4):
            side[t, 4 * ex + a] = w(a, 1 - t)

    inner = range(1, nby - 1)
    for ex in range(1, nbx - 1):
        second_elements(ex, inner)
    for t in range(2):
        arrived(0, 2 + t)
    for ex in range(nbx):
        v = inverted(ex, lambda v: with_sides(
            v, rMc[0, ex, halves_of[1], :], rMc[1, ex, halves_of[1], :]
        ))
        for y in (0, ny - 1):
            B[ex, y, halves_of[1], :] = in_all_lanes(v, y)
        for t in range(2):
            lift(rMc, (t, ex), Bc, range(4) if t else range(ny - 4, ny))
    for t in range(2):
        arrived(1, 2 + t)
    for x in range(1, nx - 1):
        for t in range(2):
            q = t * (nq - 1)
            U[x, q] = (T[x, q] + column_part(rCA, t, x)) * inverse_mass(x, q)
    for ex in range(1, nbx - 1):
        second_elements(ex, (0, nby - 1))
        for t in range(2):
            side_elements(t, ex)
    for t in range(2):
        arrived(2, 2 + t)

    def finish(x, halo=None, corner=None):
        line = [rows_sum(in_W, x, q) for q in range(nq)]
        if halo:
            line = [add(v, h) for v, h in zip(line, halo)]
        line = across(line)
        s = 0 if x == 0 else 1
        if halo:
            line = [v + rRB[s, q] for q, v in enumerate(line)]
        for t in range(2):
            q = t * (nq - 1)
            v = rows_sum(lambda x: side[t, x], x)
            if corner:
                v = v + corner[t]
            v = swap(v)
            if corner:
                last = rD[2 * s + t, 3]
                v = v + (last if t else swap(last))
            line[q] = line[q] + (high if t else low) * v + column_part(rCB, t, x)
        for at in [x] + ([x + 1] if x % 4 == 3 and x < nx - 1 else []):
            for q in range(nq):
                out_ref[at, q] = line[q] * inverse_mass(at, q)

    for x in range(5, nx - 5):
        if x % 4:
            finish(x)

    def ring_rows(s):
        xe, ex, own_row, halo_row = s * (nx - 1), s * (nbx - 1), 3 * s, 3 - 3 * s
        rest = [a for a in range(4) if a != halo_row]
        arrived(0, s)
        for t in range(2):
            arrived(0, 4 + 2 * s + t)

        own = sub == 4 + own_row
        v = inverted(ex, lambda v: with_sides(
            v + jnp.where(own, mass_row(rMr, s, halo_row), 0.0),
            *[
                rMc[t, ex, halves_of[1], :] + jnp.where(own, mass_row(rMd, 2 * s + t, halo_row), 0.0)
                for t in range(2)
            ],
        ))
        for y in range(ny):
            B[ex, y, halves_of[1], :] = in_all_lanes(v, y)
        lift(rMr, (s,), Br, range(ny))
        for t in range(2):
            lift(rMd, (2 * s + t,), Bd, range(4) if t else range(ny - 4, ny))
        inv_ext = []
        for t in range(2):
            v = 1.0 / (mass_row(rMc, t, ex, own_row) + mass_row(rMd, 2 * s + t, halo_row))
            y = (1 - t) * (ny - 4)
            inv_ext.append([
                jnp.where(is_low, in_all_lanes(v, y + 2 * p), in_all_lanes(v, y + 2 * p + 1))
                for p in range(2)
            ])
        inv_beyond = []
        for a in rest:
            v = 1.0 / with_sides(
                mass_row(rMr, s, a), mass_row(rMd, 2 * s, a), mass_row(rMd, 2 * s + 1, a)
            )
            inv_beyond.append(jnp.where(is_low, in_all_lanes(v, 0), in_all_lanes(v, ny - 1)))

        arrived(1, s)
        for t in range(2):
            arrived(1, 4 + 2 * s + t)
        for q in range(nq):
            v = T[xe, q] + rRA[s, q]
            for t in range(2):
                if q == t * (nq - 1):
                    v = v + column_part(rCA, t, xe)
                    v = v + (high if t else low) * swap(rD[2 * s + t, 1 - t])
            U[xe, q] = v * inverse_mass(xe, q)
        ext = []
        for t in range(2):
            e = [
                (rCA[t, nx // 2 + 2 * s + p] + rD[2 * s + t, p]) * inv_ext[t][p] for p in range(2)
            ]
            corner = swap(U[xe, t * (nq - 1)])
            e[1 - t] = high * e[0] + low * corner if t else low * e[1] + high * corner
            ext.append(e)
        beyond = []
        for i in range(3):
            v, w = rD[2 * s, 2 + i // 2], rD[2 * s + 1, 2 + i // 2]
            v, w = (swap(v), w) if i % 2 else (v, swap(w))
            beyond.append((rRA[s, nq + i] + low * v + high * w) * inv_beyond[i])

        second_elements(ex, range(nby))
        for t in range(2):
            side_elements(t, ex, own_row, ext[t])
        halo = []
        for ey in range(nby):
            u = [[None, None] for _ in range(4)]
            u[halo_row] = [U[xe, 2 * ey + p] for p in range(2)]
            for i, a in enumerate(rest):
                if ey == 0:
                    u[a][0] = low * beyond[i]
                if ey == nby - 1:
                    u[a][1] = high * beyond[i]
            w = laplace(u, functools.cache(lambda slot, a, p, ey=ey: tile_of(
                lambda j: Br[s, 4 * ey + j, 4 * slot + a:4 * slot + a + 1, :], p
            )))
            halo += [w(halo_row, 0), w(halo_row, 1)]
        corner = []
        for t in range(2):
            u = [[None, None] for _ in range(4)]
            u[halo_row] = ext[t]
            for i, a in enumerate(rest):
                v = swap(beyond[i])
                u[a] = [low * v, None] if t else [None, high * v]
            w = laplace(u, metrics(Bd, 2 * s + t))
            corner.append(w(halo_row, 1 - t))
        for x in (range(nx - 5, nx) if s else range(5)):
            if x % 4 and x != xe:
                finish(x)
        arrived(2, s)
        finish(xe, halo, corner)

    ring_rows(1)
    ring_rows(0)
    for copy in copies.values():
        copy.wait_send()


def solution(mesh):
    faces, cols = mesh.shape["face"], mesh.shape["col"]

    def shards(fields, metric_diag, metric_cross, point_mass):
        nf, nx, ny, lanes = fields.shape
        nbx, nby = nx // 4, ny // 4
        nq = ny // 2
        f32 = jnp.float32
        tiles = (nx, nq, 2 * nf, lanes)

        def vmem(*shape):
            return pltpu.VMEM(shape, f32)

        def messages():
            return [
                vmem(2, nq + 3, 2 * nf, lanes),
                vmem(2, nq, 2 * nf, lanes),
                vmem(2, nx // 2 + 4, 2 * nf, lanes),
                vmem(2, nx // 2, 2 * nf, lanes),
                vmem(4, 4, 2 * nf, lanes),
            ]

        out = pl.pallas_call(
            functools.partial(kernel, faces, cols, nf, nbx, nby),
            out_shape=jax.ShapeDtypeStruct(tiles, f32),
            in_specs=[pl.BlockSpec(memory_space=pltpu.HBM)] * 4,
            out_specs=pl.BlockSpec(memory_space=pltpu.VMEM),
            scratch_shapes=[
                vmem(nx, 2, ny),
                vmem(nx, ny),
                vmem(nx, ny),
                vmem(*tiles),
                vmem(*tiles),
                vmem(*tiles),
                vmem(*tiles),
                vmem(2, nx, 2 * nf, lanes),
                vmem(nbx, 16, lanes),
                vmem(nbx, ny, 16, lanes),
                vmem(2, ny, 16, lanes),
                vmem(2, nbx, 4, 16, lanes),
                vmem(4, 4, 16, lanes),
                *messages(), *messages(),
                vmem(2, 16, lanes),
                vmem(2, nbx, 16, lanes),
                vmem(4, 16, lanes),
                pltpu.SemaphoreType.DMA((3,)),
                pltpu.SemaphoreType.DMA((nbx,)),
                pltpu.SemaphoreType.DMA((3, 8)),
                pltpu.SemaphoreType.DMA((3, 8)),
                pltpu.SemaphoreType.REGULAR,
            ],
            compiler_params=pltpu.CompilerParams(
                collective_id=0, has_side_effects=True, vmem_limit_bytes=32 * 1024 * 1024
            ),
        )(*[
            pltpu.with_memory_space_constraint(v, pltpu.HBM)
            for v in (
                fields.transpose(1, 2, 0, 3).reshape(tiles),
                metric_diag.transpose(1, 0, 2), metric_cross, point_mass,
            )
        ])
        return out.reshape(nx, ny, nf, lanes).transpose(2, 0, 1, 3)

    return jax.shard_map(
        shards,
        mesh=mesh,
        in_specs=(
            P(None, "face", "col", None),
            P(None, "face", "col"),
            P("face", "col"),
            P("face", "col"),
        ),
        out_specs=P(None, "face", "col", None),
        check_vma=False,
    )
```

time: 19 us -> 16.4 us (0.86)
  Pallas kernels: 17.9 us -> 15.4 us
    pallas_call x1, Pallas kernels: 17.9 us -> 15.4 us  [shards(): pl.pallas_call(functools.partial(kernel, faces, cols, nf, nbx, nby), out_...]
where the time goes in v3:
time: 16.4 us; the launch traced here: 16.3 us
  Pallas kernels  15.4 us (94%)
  local copies, waits for them, and re-layouts  0.89 us (5%)
    pallas_call x1, Pallas kernels, shards(): pl.pallas_call(functools.partial(kernel, faces, cols, nf, nbx, nby), out_...  15.4 us
    unnamed x1, local copies, waits for them, and re-layouts  0.89 us

profile of v3, /device:TPU:0, one launch (start us, length us, event | category | flops | bytes accessed | tf_op | source)
XLA Modules:
  0.0 16.3 jit_solution(10171782255261042843)
XLA Ops:
  0.0 15.4 %shard_map.46 = f32[20,10,8,128]{3,2,1,0:T(8,128)S(1)} custom-call(f32[20,10,8,128]{3,2,1,0:T(8,128)} %bitcast.8, f32[20,2,20]{2,1,0:T(2,128)} %bitcast.9, f32[20,20]{1,0:T(8,128)} %cross_hbm.1, f32[20,20]{1,0:T(8,128)} %mass_hbm.1), custom_call_target="tpu_custom_call" | custom-call | tf_op jit(solution)/shard_map/pallas_call | solution.py:595
  15.4 0.9 %copy.6 = f32[4,20,20,128]{3,0,2,1:T(4,128)} copy(f32[4,20,20,128]{3,0,2,1:T(4,128)S(1)} %bitcast.7) | data formatting | bytes 1638400

commit v4 on v3

--- a/solution.py
+++ b/solution.py
@@ -50,8 +50,8 @@
 def kernel(
     faces, cols, nf, nbx, nby,
     fields_hbm, diag_hbm, cross_hbm, mass_hbm, out_ref,
-    diag_ref, cross_ref, mass_ref, raw, U, W, T, side, met, B, Br, Bc, Bd,
-    sRA, sRB, sCA, sCB, sD, rRA, rRB, rCA, rCB, rD, rMr, rMc, rMd,
+    diag_ref, cross_ref, mass_ref, raw, U, W, T, side, met, B, Br, Bc, Bd, inv,
+    sM, sA, sRB, sCA, sCB, rMc, rMr, rA, rRB, rCA, rCB, sent,
     small_sem, load_sem, send_sem, recv_sem, late,
 ):
     face, col = lax.axis_index("face"), lax.axis_index("col")
@@ -74,23 +74,17 @@
     nx, ny, nq = 4 * nbx, 4 * nby, 2 * nby
     lanes = raw.shape[-1]
     tile = (2 * nf, lanes)
-    order = [nbx - 1, nbx - 2] + list(range(nbx - 2))
+    corner_at = [nq + 3, nq + 7]
     small = [
         pltpu.make_async_copy(src, dst, small_sem.at[k])
         for k, (src, dst) in enumerate(
             ((diag_hbm, diag_ref), (cross_hbm, cross_ref), (mass_hbm, mass_ref))
         )
     ]
-    loads = {
-        ex: pltpu.make_async_copy(
-            fields_hbm.at[pl.ds(4 * ex, 4)], raw.at[pl.ds(4 * ex, 4)], load_sem.at[ex]
-        )
-        for ex in order
-    }
+    load = pltpu.make_async_copy(fields_hbm, raw, load_sem)
     for copy in small:
         copy.start()
-    for ex in order:
-        loads[ex].start()
+    load.start()
 
     D = derivative_table()
     is_low = lax.broadcasted_iota(jnp.int32, tile, 0) < nf
@@ -173,32 +167,43 @@
     def inverse_mass(x, q):
         return own_metrics(x // 4, q // 2)(3, x % 4, q % 2)
 
-    def send(phase, k, src, dst, start=True):
-        copy = pltpu.make_async_remote_copy(
-            src_ref=src, dst_ref=dst,
-            send_sem=send_sem.at[phase, k], recv_sem=recv_sem.at[phase, opposite[k]],
+    def copy_of(group, k, src, dst):
+        return pltpu.make_async_remote_copy(
+            src_ref=src, dst_ref=dst, send_sem=send_sem, recv_sem=recv_sem.at[group],
             device_id=peers[k], device_id_type=MESH,
         )
-        if start:
+
+    def arrived(group, landed):
+        pltpu.make_async_remote_copy(
+            src_ref=landed, dst_ref=landed, send_sem=send_sem, recv_sem=recv_sem.at[group],
+            device_id=peers[0], device_id_type=MESH,
+        ).wait_recv()
+
+    def row_metrics(s):
+        return [copy_of(3 + 3 * (1 - s), s, sM.at[s], rMr.at[1 - s, 0])] + [
+            copy_of(3 + 3 * (1 - s), 4 + 2 * s + t, sM.at[s], rMr.at[1 - s, 2 - t]) for t in range(2)
+        ]
+
+    def row_edges(s):
+        return copy_of(
+            4 + 3 * (1 - s), s, sA.at[s, pl.ds(0, nq + 3)], rA.at[1 - s, pl.ds(0, nq + 3)]
+        )
+
+    def row_corners(s):
+        return [
+            copy_of(
+                4 + 3 * (1 - s), 4 + 2 * s + t,
+                sA.at[s, pl.ds(corner_at[t], 4)], rA.at[1 - s, pl.ds(corner_at[1 - t], 4)],
+            )
+            for t in range(2)
+        ]
+
+    def row_parts(s):
+        return copy_of(5 + 3 * (1 - s), s, sRB.at[s], rRB.at[1 - s])
+
+    def start(*those):
+        for copy in those:
             copy.start()
-        copies[phase, k] = copy
-        return copy
-
-    def arrived(phase, k):
-        copies[phase, opposite[k]].wait_recv()
-
-    held = []
-
-    def send_back(*those):
-        made = [send(*one, start=False) for one in those]
-        held.extend(made)
-
-        @pl.when(face != 0)
-        def _():
-            for copy in made:
-                copy.start()
-
-    copies = {}
 
     for copy in small:
         copy.wait()
@@ -217,38 +222,38 @@
         for ex in range(nbx):
             met[ex, 4 * slot:4 * slot + 4, :ny] = v[4 * ex:4 * ex + 4]
 
-    pl.semaphore_wait(barrier, jnp.where(face == 0, 5, 8))
-
-    @pl.when(face == faces - 1)
-    def _():
-        for k in after:
-            pl.semaphore_signal(late, inc=1, device_id=peers[k], device_id_type=MESH)
-
-    send(0, 1, met.at[nbx - 1], rMr.at[0])
-    for t in range(2):
-        send(0, 6 + t, met.at[nbx - 1], rMd.at[1 - t])
-    for t in range(2):
-        send(0, 2 + t, met, rMc.at[1 - t])
-    send_back((0, 0, met.at[0], rMr.at[1]), (0, 4, met.at[0], rMd.at[3]), (0, 5, met.at[0], rMd.at[2]))
-
     sub = lax.broadcasted_iota(jnp.int32, tile, 0)
     halves_of = [pl.ds(8 * i, 8) for i in range(2)]
+
+    half_lanes = 32
+
+    def side_by_side(v, w):
+        return jnp.where(lane < half_lanes, v, pltpu.roll(w, half_lanes, 1))
+
+    for s in range(2):
+        sM[s] = side_by_side(*[met[s * (nbx - 1), half, :] for half in halves_of])
+    for t in range(2):
+        packed = [jnp.zeros(tile, jnp.float32)] * 2
+        for ex in range(nbx):
+            for i, half in enumerate(halves_of):
+                v = pltpu.roll(met[ex, half, :], (4 * ex - t * (ny - 4)) % lanes, 1)
+                packed[i] = jnp.where((lane >= 4 * ex) & (lane < 4 * ex + 4), v, packed[i])
+        sM[2 + t] = side_by_side(*packed)
 
     def inverted(ex, mass_of=lambda v: v):
         v = met[ex, halves_of[1], :]
         return jnp.where(sub < 4, v, 1.0 / mass_of(v))
 
-    for ex in order:
+    for ex in range(nbx):
         v, w = met[ex, halves_of[0], :], inverted(ex)
         for y in range(ny):
             B[ex, y, halves_of[0], :] = in_all_lanes(v, y)
             B[ex, y, halves_of[1], :] = in_all_lanes(w, y)
 
-    def lift(ref, at, to, ys):
-        for half in halves_of:
-            v = ref[(*at, half)]
-            for i, y in enumerate(ys):
-                to[(*at, i, half)] = in_all_lanes(v, y)
+    def lift(v, to, at, lane_of):
+        for i, y in enumerate(lane_of):
+            for h, half in enumerate(halves_of):
+                to[(*at, i, half)] = in_all_lanes(v, y + h * half_lanes)
 
     def rows_sum(src, x, *at):
         if x % 4 == 0 and x > 0:
@@ -267,7 +272,6 @@
         return W[x, q]
 
     def first_laplacian(ex):
-        loads[ex].wait()
         for ey in range(nby):
             w = laplace(
                 [[raw[4 * ex + a, 2 * ey + p] for p in range(2)] for a in range(4)],
@@ -293,7 +297,7 @@
                 v = T[x, q] * inverse_mass(x, q)
                 U[x, q] = high * v if q == 0 else low * v if q == nq - 1 else v
 
-    def known(ex, ey):
+    def known_values(ex, ey):
         return [
             [None if x in (0, nx - 1) else U[x, 2 * ey + p] for p in range(2)]
             for x in range(4 * ex, 4 * ex + 4)
@@ -305,7 +309,7 @@
         for ey in range(nby):
             if edge is None and 0 < ey < nby - 1:
                 continue
-            w = laplace(known(ex, ey), own_metrics(ex, ey))
+            w = laplace(known_values(ex, ey), own_metrics(ex, ey))
             if edge:
                 line[2 * ey], line[2 * ey + 1] = w(edge[1], 0), w(edge[1], 1)
             for t, e in ((0, 0), (1, nby - 1)):
@@ -320,80 +324,112 @@
     def stage_row(s):
         xe, near = s * (nx - 1), (nx - 4 if s else 1)
         for q in range(nq):
-            sRA[s, q] = T[xe, q]
+            sA[s, q] = T[xe, q]
         for i in range(3):
-            sRA[s, nq + i] = jnp.where(is_low, T[near + i, 0], T[near + i, nq - 1])
+            sA[s, nq + i] = jnp.where(is_low, T[near + i, 0], T[near + i, nq - 1])
 
     def stage_corner(s, t):
         xe, near, q = s * (nx - 1), (nx - 4 if s else 1), t * (nq - 1)
         for p in range(2):
-            sD[2 * s + t, p] = T[xe, t * (nq - 2) + p]
+            sA[s, corner_at[t] + p] = T[xe, t * (nq - 2) + p]
         halves = [T[near + i, q] for i in range(3)] + [sRB[s, q]]
         for i in range(2):
-            v, w = halves[2 * i], halves[2 * i + 1]
-            sD[2 * s + t, 2 + i] = (
-                jnp.where(is_low, swap(v), w) if t else jnp.where(is_low, v, swap(w))
-            )
+            sA[s, corner_at[t] + 2 + i] = pack_column(t, halves[2 * i], halves[2 * i + 1])
 
     def pack_column(t, v, w):
         return jnp.where(is_low, swap(v), w) if t else jnp.where(is_low, v, swap(w))
 
-    for ex in order[:2]:
-        first_laplacian(ex)
-    first_rows(range(nx - 5, nx))
-    stage_row(1)
-    send(1, 1, sRA.at[1], rRA.at[0])
-    inner_first(range(nx - 4, nx - 1))
-    known_parts(nbx - 1)
-    for t in range(2):
-        stage_corner(1, t)
-        send(1, 6 + t, sD.at[2 + t], rD.at[1 - t])
-    send(2, 1, sRB.at[1], rRB.at[0])
-
-    for ex in order[2:]:
-        first_laplacian(ex)
-    first_rows(range(nx - 5))
-    for t in range(2):
-        q = t * (nq - 1)
-        for k in range(nx // 2):
-            sCA[t, k] = pack_column(t, T[2 * k, q], T[2 * k + 1, q])
-        for s in range(2):
-            for p in range(2):
-                sCA[t, nx // 2 + 2 * s + p] = T[s * (nx - 1), t * (nq - 2) + p]
-        send(1, 2 + t, sCA.at[t], rCA.at[1 - t])
-    stage_row(0)
-    send_back((1, 0, sRA.at[0], rRA.at[1]))
-    inner_first(range(1, nx - 4))
-    for ex in range(nbx - 1):
-        known_parts(ex)
-    for t in range(2):
-        stage_corner(0, t)
-    send_back(
-        (1, 4, sD.at[0], rD.at[3]), (1, 5, sD.at[1], rD.at[2]), (2, 0, sRB.at[0], rRB.at[1])
-    )
-    for t in range(2):
-        def in_side(x, t=t):
-            return side[t, x]
-
-        for k in range(nx // 2):
-            sCB[t, k] = pack_column(t, rows_sum(in_side, 2 * k), rows_sum(in_side, 2 * k + 1))
-        send(2, 2 + t, sCB.at[t], rCB.at[1 - t])
+    def exchange(first, hold=False):
+        near, far = (lambda s: s * (nbx - 1)), (lambda s: 1 + s * (nbx - 3))
+        rows = [range(4), range(nx - 5, nx)]
+        edge_rows = [range(1, 4), range(nx - 4, nx - 1)]
+        other = 1 - first
+        columns = [copy_of(0, 2 + t, sM.at[2 + t], rMc.at[1 - t]) for t in range(2)]
+        waiting = []
+
+        def launch(*those):
+            if hold:
+                waiting.extend(those)
+            else:
+                start(*those)
+
+        first_laplacian(near(first))
+        first_laplacian(far(first))
+        first_rows(rows[first])
+        stage_row(first)
+        if not hold:
+            pl.semaphore_wait(barrier, 8)
+            if first:
+                @pl.when(face == faces - 1)
+                def _():
+                    for k in after:
+                        pl.semaphore_signal(late, inc=1, device_id=peers[k], device_id_type=MESH)
+        launch(*row_metrics(first), row_edges(first), *columns)
+
+        def known(s):
+            inner_first(edge_rows[s])
+            known_parts(near(s))
+            for t in range(2):
+                stage_corner(s, t)
+
+        known(first)
+        launch(*row_corners(first), row_parts(first))
+        for ex in range(nbx):
+            if ex not in (near(first), far(first)):
+                first_laplacian(ex)
+        first_rows(range(5, nx - 5))
+        first_rows(rows[other])
+        for t in range(2):
+            q = t * (nq - 1)
+            for k in range(nx // 2):
+                sCA[t, k] = pack_column(t, T[2 * k, q], T[2 * k + 1, q])
+            for s in range(2):
+                for p in range(2):
+                    sCA[t, nx // 2 + 2 * s + p] = T[s * (nx - 1), t * (nq - 2) + p]
+            launch(copy_of(1, 2 + t, sCA.at[t], rCA.at[1 - t]))
+        stage_row(other)
+        known(other)
+        inner_first(range(4, nx - 4))
+        for ex in range(1, nbx - 1):
+            known_parts(ex)
+        for t in range(2):
+            def in_side(x, t=t):
+                return side[t, x]
+
+            for k in range(nx // 2):
+                sCB[t, k] = pack_column(t, rows_sum(in_side, 2 * k), rows_sum(in_side, 2 * k + 1))
+            launch(copy_of(2, 2 + t, sCB.at[t], rCB.at[1 - t]))
+        if hold:
+            pl.semaphore_wait(barrier, 5)
+            start(*waiting)
+        else:
+            start(*row_metrics(other), row_edges(other), *row_corners(other), row_parts(other))
+
+    load.wait()
 
     @pl.when(face == 0)
     def _():
-        pl.semaphore_wait(late, 3)
-        for copy in held:
-            copy.start()
-
-    def mass_row(ref, *at):
-        return wide(ref[(*at[:-1], pl.ds(12 + at[-1], 1))])
-
-    def with_sides(mid, left, right):
-        return (
-            mid
-            + jnp.where(lane == 0, pltpu.roll(left, lanes - (ny - 1), 1), 0.0)
-            + jnp.where(lane == ny - 1, pltpu.roll(right, ny - 1, 1), 0.0)
-        )
+        exchange(1, hold=True)
+
+    @pl.when((face > 0) & (face < faces // 2))
+    def _():
+        exchange(0)
+
+    @pl.when(face >= faces // 2)
+    def _():
+        exchange(1)
+
+    def turned(v, shift):
+        return pltpu.roll(v, shift % lanes, 1)
+
+    def mass_row(v, a):
+        return wide(v[4 + a:5 + a, :])
+
+    def at_ends(left, right):
+        return jnp.where(lane == 0, left, 0.0) + jnp.where(lane == ny - 1, right, 0.0)
+
+    def column_masses(t, ex):
+        return turned(rMc[t], t * (ny - 1) - (half_lanes + 4 * ex + 3 * (1 - t)))
 
     def column_part(ref, t, x):
         v = ref[t, x // 2]
@@ -425,18 +461,14 @@
     inner = range(1, nby - 1)
     for ex in range(1, nbx - 1):
         second_elements(ex, inner)
-    for t in range(2):
-        arrived(0, 2 + t)
+    arrived(0, rMc)
     for ex in range(nbx):
-        v = inverted(ex, lambda v: with_sides(
-            v, rMc[0, ex, halves_of[1], :], rMc[1, ex, halves_of[1], :]
-        ))
+        v = inverted(ex, lambda v: v + at_ends(column_masses(0, ex), column_masses(1, ex)))
         for y in (0, ny - 1):
             B[ex, y, halves_of[1], :] = in_all_lanes(v, y)
         for t in range(2):
-            lift(rMc, (t, ex), Bc, range(4) if t else range(ny - 4, ny))
-    for t in range(2):
-        arrived(1, 2 + t)
+            lift(rMc[t], Bc, (t, ex), range(4 * ex, 4 * ex + 4))
+    arrived(1, rCA)
     for x in range(1, nx - 1):
         for t in range(2):
             q = t * (nq - 1)
@@ -445,17 +477,19 @@
         second_elements(ex, (0, nby - 1))
         for t in range(2):
             side_elements(t, ex)
-    for t in range(2):
-        arrived(2, 2 + t)
-
-    def finish(x, halo=None, corner=None):
+
+    @pl.when(face == 0)
+    def _():
+        pl.semaphore_wait(late, 3)
+        start(*row_metrics(0), row_edges(0), *row_corners(0), row_parts(0))
+
+    arrived(2, rCB)
+
+    def summed(x, halo=None, corner=None):
         line = [rows_sum(in_W, x, q) for q in range(nq)]
         if halo:
             line = [add(v, h) for v, h in zip(line, halo)]
         line = across(line)
-        s = 0 if x == 0 else 1
-        if halo:
-            line = [v + rRB[s, q] for q, v in enumerate(line)]
         for t in range(2):
             q = t * (nq - 1)
             v = rows_sum(lambda x: side[t, x], x)
@@ -463,9 +497,16 @@
                 v = v + corner[t]
             v = swap(v)
             if corner:
-                last = rD[2 * s + t, 3]
+                last = rA[s_of(x), corner_at[t] + 3]
                 v = v + (last if t else swap(last))
             line[q] = line[q] + (high if t else low) * v + column_part(rCB, t, x)
+        return line
+
+    def s_of(x):
+        return 0 if x == 0 else 1
+
+    def finish(x):
+        line = summed(x)
         for at in [x] + ([x + 1] if x % 4 == 3 and x < nx - 1 else []):
             for q in range(nq):
                 out_ref[at, q] = line[q] * inverse_mass(at, q)
@@ -474,64 +515,64 @@
         if x % 4:
             finish(x)
 
+    def ring_metrics(s):
+        ex, own_row, halo_row = s * (nbx - 1), 3 * s, 3 - 3 * s
+        arrived(3 + 3 * s, rMr.at[s])
+        beyond = [turned(rMr[s, k], -half_lanes) for k in range(3)]
+        own = sub == 4 + own_row
+        ends = [
+            column_masses(t, ex)
+            + jnp.where(own, mass_row(turned(beyond[1 + t], (2 * t - 1) * (ny - 1)), halo_row), 0.0)
+            for t in range(2)
+        ]
+        v = inverted(ex, lambda v: (
+            v + jnp.where(own, mass_row(beyond[0], halo_row), 0.0) + at_ends(*ends)
+        ))
+        for y in range(ny):
+            B[ex, y, halves_of[1], :] = in_all_lanes(v, y)
+        lift(rMr[s, 0], Br, (s,), range(ny))
+        for t in range(2):
+            lift(rMr[s, 1 + t], Bd, (2 * s + t,), range(4) if t else range(ny - 4, ny))
+            v = 1.0 / (
+                mass_row(turned(rMc[t], -(half_lanes + 4 * ex)), own_row)
+                + mass_row(turned(beyond[1 + t], 0 if t else -(ny - 4)), halo_row)
+            )
+            for p in range(2):
+                inv[s, 2 * t + p] = jnp.where(
+                    is_low, in_all_lanes(v, 2 * p), in_all_lanes(v, 2 * p + 1)
+                )
+        v = 1.0 / (beyond[0] + at_ends(
+            turned(beyond[1], -(ny - 1)), turned(beyond[2], ny - 1)
+        ))
+        for i in range(3):
+            row = mass_row(v, i + s)
+            inv[s, 4 + i] = jnp.where(is_low, in_all_lanes(row, 0), in_all_lanes(row, ny - 1))
+
     def ring_rows(s):
         xe, ex, own_row, halo_row = s * (nx - 1), s * (nbx - 1), 3 * s, 3 - 3 * s
         rest = [a for a in range(4) if a != halo_row]
-        arrived(0, s)
-        for t in range(2):
-            arrived(0, 4 + 2 * s + t)
-
-        own = sub == 4 + own_row
-        v = inverted(ex, lambda v: with_sides(
-            v + jnp.where(own, mass_row(rMr, s, halo_row), 0.0),
-            *[
-                rMc[t, ex, halves_of[1], :] + jnp.where(own, mass_row(rMd, 2 * s + t, halo_row), 0.0)
-                for t in range(2)
-            ],
-        ))
-        for y in range(ny):
-            B[ex, y, halves_of[1], :] = in_all_lanes(v, y)
-        lift(rMr, (s,), Br, range(ny))
-        for t in range(2):
-            lift(rMd, (2 * s + t,), Bd, range(4) if t else range(ny - 4, ny))
-        inv_ext = []
-        for t in range(2):
-            v = 1.0 / (mass_row(rMc, t, ex, own_row) + mass_row(rMd, 2 * s + t, halo_row))
-            y = (1 - t) * (ny - 4)
-            inv_ext.append([
-                jnp.where(is_low, in_all_lanes(v, y + 2 * p), in_all_lanes(v, y + 2 * p + 1))
-                for p in range(2)
-            ])
-        inv_beyond = []
-        for a in rest:
-            v = 1.0 / with_sides(
-                mass_row(rMr, s, a), mass_row(rMd, 2 * s, a), mass_row(rMd, 2 * s + 1, a)
-            )
-            inv_beyond.append(jnp.where(is_low, in_all_lanes(v, 0), in_all_lanes(v, ny - 1)))
-
-        arrived(1, s)
-        for t in range(2):
-            arrived(1, 4 + 2 * s + t)
+        arrived(4 + 3 * s, rA.at[s])
         for q in range(nq):
-            v = T[xe, q] + rRA[s, q]
+            v = T[xe, q] + rA[s, q]
             for t in range(2):
                 if q == t * (nq - 1):
                     v = v + column_part(rCA, t, xe)
-                    v = v + (high if t else low) * swap(rD[2 * s + t, 1 - t])
+                    v = v + (high if t else low) * swap(rA[s, corner_at[t] + 1 - t])
             U[xe, q] = v * inverse_mass(xe, q)
         ext = []
         for t in range(2):
             e = [
-                (rCA[t, nx // 2 + 2 * s + p] + rD[2 * s + t, p]) * inv_ext[t][p] for p in range(2)
+                (rCA[t, nx // 2 + 2 * s + p] + rA[s, corner_at[t] + p]) * inv[s, 2 * t + p]
+                for p in range(2)
             ]
             corner = swap(U[xe, t * (nq - 1)])
             e[1 - t] = high * e[0] + low * corner if t else low * e[1] + high * corner
             ext.append(e)
         beyond = []
         for i in range(3):
-            v, w = rD[2 * s, 2 + i // 2], rD[2 * s + 1, 2 + i // 2]
+            v, w = [rA[s, at + 2 + i // 2] for at in corner_at]
             v, w = (swap(v), w) if i % 2 else (v, swap(w))
-            beyond.append((rRA[s, nq + i] + low * v + high * w) * inv_beyond[i])
+            beyond.append((rA[s, nq + i] + low * v + high * w) * inv[s, 4 + i])
 
         second_elements(ex, range(nby))
         for t in range(2):
@@ -561,13 +602,36 @@
         for x in (range(nx - 5, nx) if s else range(5)):
             if x % 4 and x != xe:
                 finish(x)
-        arrived(2, s)
-        finish(xe, halo, corner)
+        line = summed(xe, halo, corner)
+        for q in range(nq):
+            T[xe, q] = line[q]
+
+    def last_row(s):
+        xe = s * (nx - 1)
+        arrived(5 + 3 * s, rRB.at[s])
+        for q in range(nq):
+            out_ref[xe, q] = (T[xe, q] + rRB[s, q]) * inverse_mass(xe, q)
+
+
+    ring_metrics(1)
+
+    @pl.when(face != 0)
+    def _():
+        ring_metrics(0)
 
     ring_rows(1)
+
+    @pl.when(face == 0)
+    def _():
+        ring_metrics(0)
+
     ring_rows(0)
-    for copy in copies.values():
-        copy.wait_send()
+    last_row(1)
+    last_row(0)
+    pltpu.make_async_remote_copy(
+        src_ref=sent, dst_ref=sent, send_sem=send_sem, recv_sem=recv_sem.at[0],
+        device_id=peers[0], device_id_type=MESH,
+    ).wait_send()
 
 
 def solution(mesh):
@@ -585,13 +649,13 @@
 
         def messages():
             return [
-                vmem(2, nq + 3, 2 * nf, lanes),
+                vmem(2, nq + 3 + 8, 2 * nf, lanes),
                 vmem(2, nq, 2 * nf, lanes),
                 vmem(2, nx // 2 + 4, 2 * nf, lanes),
                 vmem(2, nx // 2, 2 * nf, lanes),
-                vmem(4, 4, 2 * nf, lanes),
             ]
 
+        tiles_sent = 2 * (2 * nq + 3 + 4) + 2 * (nx + 4) + 8 + 8
         out = pl.pallas_call(
             functools.partial(kernel, faces, cols, nf, nbx, nby),
             out_shape=jax.ShapeDtypeStruct(tiles, f32),
@@ -611,14 +675,17 @@
                 vmem(2, ny, 16, lanes),
                 vmem(2, nbx, 4, 16, lanes),
                 vmem(4, 4, 16, lanes),
-                *messages(), *messages(),
-                vmem(2, 16, lanes),
-                vmem(2, nbx, 16, lanes),
-                vmem(4, 16, lanes),
+                vmem(2, 7, 2 * nf, lanes),
+                vmem(4, 2 * nf, lanes),
+                *messages(),
+                vmem(2, 2 * nf, lanes),
+                vmem(2, 3, 2 * nf, lanes),
+                *messages(),
+                vmem(tiles_sent, 2 * nf, lanes),
                 pltpu.SemaphoreType.DMA((3,)),
-                pltpu.SemaphoreType.DMA((nbx,)),
-                pltpu.SemaphoreType.DMA((3, 8)),
-                pltpu.SemaphoreType.DMA((3, 8)),
+                pltpu.SemaphoreType.DMA,
+                pltpu.SemaphoreType.DMA,
+                pltpu.SemaphoreType.DMA((9,)),
                 pltpu.SemaphoreType.REGULAR,
             ],
             compiler_params=pltpu.CompilerParams(

time: 16.4 us -> 13.6 us (0.83)
  Pallas kernels: 15.4 us -> 12.5 us
    pallas_call x1, Pallas kernels: 15.4 us -> 12.5 us  [shards(): pl.pallas_call(functools.partial(kernel, faces, cols, nf, nbx, nby), out_...]
where the time goes in v4:
time: 13.6 us; the launch traced here: 13.4 us
  Pallas kernels  12.5 us (92%)
  local copies, waits for them, and re-layouts  0.89 us (7%)
    pallas_call x1, Pallas kernels, shards(): pl.pallas_call(functools.partial(kernel, faces, cols, nf, nbx, nby), out_...  12.5 us
    unnamed x1, local copies, waits for them, and re-layouts  0.89 us

profile of v4, /device:TPU:0, one launch (start us, length us, event | category | flops | bytes accessed | tf_op | source)
XLA Modules:
  0.0 13.4 jit_solution(11839549037288423656)
XLA Ops:
  0.0 12.5 %shard_map.46 = f32[20,10,8,128]{3,2,1,0:T(8,128)S(1)} custom-call(f32[20,10,8,128]{3,2,1,0:T(8,128)} %bitcast.8, f32[20,2,20]{2,1,0:T(2,128)} %bitcast.9, f32[20,20]{1,0:T(8,128)} %cross_hbm.1, f32[20,20]{1,0:T(8,128)} %mass_hbm.1), custom_call_target="tpu_custom_call" | custom-call | tf_op jit(solution)/shard_map/pallas_call | solution.py:659
  12.5 0.9 %copy.6 = f32[4,20,20,128]{3,0,2,1:T(4,128)} copy(f32[4,20,20,128]{3,0,2,1:T(4,128)S(1)} %bitcast.7) | data formatting | bytes 1638400

commit v5 on v4

--- a/solution.py
+++ b/solution.py
@@ -63,13 +63,13 @@
     before, after = [0, 4, 5], [1, 6, 7]
 
     barrier = pltpu.get_barrier_semaphore()
-    for k in (2, 3, *before):
+    for k in (2, 3):
         pl.semaphore_signal(barrier, inc=1, device_id=peers[k], device_id_type=MESH)
-
-    @pl.when(face != faces - 1)
-    def _():
-        for k in after:
-            pl.semaphore_signal(barrier, inc=1, device_id=peers[k], device_id_type=MESH)
+    for on_time, those in (((face < 1) | (face > 2), before), (face != faces - 1, after)):
+        @pl.when(on_time)
+        def _():
+            for k in those:
+                pl.semaphore_signal(barrier, inc=1, device_id=peers[k], device_id_type=MESH)
 
     nx, ny, nq = 4 * nbx, 4 * nby, 2 * nby
     lanes = raw.shape[-1]
@@ -184,10 +184,8 @@
             copy_of(3 + 3 * (1 - s), 4 + 2 * s + t, sM.at[s], rMr.at[1 - s, 2 - t]) for t in range(2)
         ]
 
-    def row_edges(s):
-        return copy_of(
-            4 + 3 * (1 - s), s, sA.at[s, pl.ds(0, nq + 3)], rA.at[1 - s, pl.ds(0, nq + 3)]
-        )
+    def row_edges(s, at, size):
+        return copy_of(4 + 3 * (1 - s), s, sA.at[s, pl.ds(at, size)], rA.at[1 - s, pl.ds(at, size)])
 
     def row_corners(s):
         return [
@@ -200,6 +198,9 @@
 
     def row_parts(s):
         return copy_of(5 + 3 * (1 - s), s, sRB.at[s], rRB.at[1 - s])
+
+    def all_to(s):
+        return [*row_metrics(s), row_edges(s, 0, nq + 3), *row_corners(s), row_parts(s)]
 
     def start(*those):
         for copy in those:
@@ -244,7 +245,7 @@
         v = met[ex, halves_of[1], :]
         return jnp.where(sub < 4, v, 1.0 / mass_of(v))
 
-    for ex in range(nbx):
+    def lift_own(ex):
         v, w = met[ex, halves_of[0], :], inverted(ex)
         for y in range(ny):
             B[ex, y, halves_of[0], :] = in_all_lanes(v, y)
@@ -272,6 +273,7 @@
         return W[x, q]
 
     def first_laplacian(ex):
+        lift_own(ex)
         for ey in range(nby):
             w = laplace(
                 [[raw[4 * ex + a, 2 * ey + p] for p in range(2)] for a in range(4)],
@@ -321,17 +323,17 @@
             for q in range(nq):
                 sRB[edge[0], q] = line[q]
 
-    def stage_row(s):
-        xe, near = s * (nx - 1), (nx - 4 if s else 1)
+    def stage_edge(s):
         for q in range(nq):
-            sA[s, q] = T[xe, q]
-        for i in range(3):
-            sA[s, nq + i] = jnp.where(is_low, T[near + i, 0], T[near + i, nq - 1])
+            sA[s, q] = T[s * (nx - 1), q]
 
     def stage_corner(s, t):
         xe, near, q = s * (nx - 1), (nx - 4 if s else 1), t * (nq - 1)
         for p in range(2):
             sA[s, corner_at[t] + p] = T[xe, t * (nq - 2) + p]
+        if t == 0:
+            for i in range(3):
+                sA[s, nq + i] = jnp.where(is_low, T[near + i, 0], T[near + i, nq - 1])
         halves = [T[near + i, q] for i in range(3)] + [sRB[s, q]]
         for i in range(2):
             sA[s, corner_at[t] + 2 + i] = pack_column(t, halves[2 * i], halves[2 * i + 1])
@@ -341,30 +343,29 @@
 
     def exchange(first, hold=False):
         near, far = (lambda s: s * (nbx - 1)), (lambda s: 1 + s * (nbx - 3))
-        rows = [range(4), range(nx - 5, nx)]
+        rows = [range(3), range(nx - 3, nx)]
+        pair = [3, nx - 5]
         edge_rows = [range(1, 4), range(nx - 4, nx - 1)]
         other = 1 - first
         columns = [copy_of(0, 2 + t, sM.at[2 + t], rMc.at[1 - t]) for t in range(2)]
-        waiting = []
-
-        def launch(*those):
-            if hold:
-                waiting.extend(those)
-            else:
-                start(*those)
 
         first_laplacian(near(first))
+        first_rows(rows[first])
+        stage_edge(first)
+        if not hold:
+            pl.semaphore_wait(barrier, 8 if first else jnp.where(face == 1, 5, 8))
+            start(*row_metrics(first), row_edges(first, 0, nq), *columns)
+            are_late, those = ((face <= 2, before), (face == faces - 1, after))[first]
+
+            @pl.when(are_late)
+            def _():
+                for k in those:
+                    pl.semaphore_signal(
+                        late.at[1 - first], inc=1, device_id=peers[k], device_id_type=MESH
+                    )
+
         first_laplacian(far(first))
-        first_rows(rows[first])
-        stage_row(first)
-        if not hold:
-            pl.semaphore_wait(barrier, 8)
-            if first:
-                @pl.when(face == faces - 1)
-                def _():
-                    for k in after:
-                        pl.semaphore_signal(late, inc=1, device_id=peers[k], device_id_type=MESH)
-        launch(*row_metrics(first), row_edges(first), *columns)
+        first_rows([pair[first]])
 
         def known(s):
             inner_first(edge_rows[s])
@@ -373,12 +374,16 @@
                 stage_corner(s, t)
 
         known(first)
-        launch(*row_corners(first), row_parts(first))
+        if not hold:
+            start(row_edges(first, nq, 3), *row_corners(first), row_parts(first))
         for ex in range(nbx):
             if ex not in (near(first), far(first)):
                 first_laplacian(ex)
         first_rows(range(5, nx - 5))
-        first_rows(rows[other])
+        first_rows([*rows[other], pair[other]])
+        if hold:
+            pl.semaphore_wait(barrier, 2)
+            start(*columns)
         for t in range(2):
             q = t * (nq - 1)
             for k in range(nx // 2):
@@ -386,9 +391,19 @@
             for s in range(2):
                 for p in range(2):
                     sCA[t, nx // 2 + 2 * s + p] = T[s * (nx - 1), t * (nq - 2) + p]
-            launch(copy_of(1, 2 + t, sCA.at[t], rCA.at[1 - t]))
-        stage_row(other)
+            start(copy_of(1, 2 + t, sCA.at[t], rCA.at[1 - t]))
+        def to_other(*those):
+            if other:
+                @pl.when(face > 1)
+                def _():
+                    start(*those)
+            elif not hold:
+                start(*those)
+
+        stage_edge(other)
+        to_other(*row_metrics(other), row_edges(other, 0, nq))
         known(other)
+        to_other(row_edges(other, nq, 3), *row_corners(other), row_parts(other))
         inner_first(range(4, nx - 4))
         for ex in range(1, nbx - 1):
             known_parts(ex)
@@ -398,12 +413,12 @@
 
             for k in range(nx // 2):
                 sCB[t, k] = pack_column(t, rows_sum(in_side, 2 * k), rows_sum(in_side, 2 * k + 1))
-            launch(copy_of(2, 2 + t, sCB.at[t], rCB.at[1 - t]))
-        if hold:
-            pl.semaphore_wait(barrier, 5)
-            start(*waiting)
-        else:
-            start(*row_metrics(other), row_edges(other), *row_corners(other), row_parts(other))
+            start(copy_of(2, 2 + t, sCB.at[t], rCB.at[1 - t]))
+        if other:
+            @pl.when(face == 1)
+            def _():
+                pl.semaphore_wait(late.at[1], 3)
+                start(*all_to(1))
 
     load.wait()
 
@@ -411,11 +426,11 @@
     def _():
         exchange(1, hold=True)
 
-    @pl.when((face > 0) & (face < faces // 2))
+    @pl.when((face > 0) & (face < faces - 1))
     def _():
         exchange(0)
 
-    @pl.when(face >= faces // 2)
+    @pl.when(face >= faces - 1)
     def _():
         exchange(1)
 
@@ -480,8 +495,10 @@
 
     @pl.when(face == 0)
     def _():
-        pl.semaphore_wait(late, 3)
-        start(*row_metrics(0), row_edges(0), *row_corners(0), row_parts(0))
+        pl.semaphore_wait(late.at[1], 3)
+        start(*all_to(1))
+        pl.semaphore_wait(late.at[0], 3)
+        start(*all_to(0))
 
     arrived(2, rCB)
 
@@ -686,7 +703,7 @@
                 pltpu.SemaphoreType.DMA,
                 pltpu.SemaphoreType.DMA,
                 pltpu.SemaphoreType.DMA((9,)),
-                pltpu.SemaphoreType.REGULAR,
+                pltpu.SemaphoreType.REGULAR((2,)),
             ],
             compiler_params=pltpu.CompilerParams(
                 collective_id=0, has_side_effects=True, vmem_limit_bytes=32 * 1024 * 1024

time: 13.6 us -> 12.9 us (0.949)
  Pallas kernels: 12.5 us -> 11.9 us
    pallas_call x1, Pallas kernels: 12.5 us -> 11.9 us  [shards(): pl.pallas_call(functools.partial(kernel, faces, cols, nf, nbx, nby), out_...]
where the time goes in v5:
time: 12.9 us; the launch traced here: 12.8 us
  Pallas kernels  11.9 us (92%)
  local copies, waits for them, and re-layouts  0.89 us (7%)
    pallas_call x1, Pallas kernels, shards(): pl.pallas_call(functools.partial(kernel, faces, cols, nf, nbx, nby), out_...  11.9 us
    unnamed x1, local copies, waits for them, and re-layouts  0.89 us

profile of v5, /device:TPU:0, one launch (start us, length us, event | category | flops | bytes accessed | tf_op | source)
XLA Modules:
  0.0 12.8 jit_solution(1473002660225685430)
XLA Ops:
  0.0 11.9 %shard_map.46 = f32[20,10,8,128]{3,2,1,0:T(8,128)S(1)} custom-call(f32[20,10,8,128]{3,2,1,0:T(8,128)} %bitcast.8, f32[20,2,20]{2,1,0:T(2,128)} %bitcast.9, f32[20,20]{1,0:T(8,128)} %cross_hbm.1, f32[20,20]{1,0:T(8,128)} %mass_hbm.1), custom_call_target="tpu_custom_call" | custom-call | tf_op jit(solution)/shard_map/pallas_call | solution.py:676
  11.9 0.9 %copy.6 = f32[4,20,20,128]{3,0,2,1:T(4,128)} copy(f32[4,20,20,128]{3,0,2,1:T(4,128)S(1)} %bitcast.7) | data formatting | bytes 1638400

commit v6 on v5

--- a/solution.py
+++ b/solution.py
@@ -51,7 +51,7 @@
     faces, cols, nf, nbx, nby,
     fields_hbm, diag_hbm, cross_hbm, mass_hbm, out_ref,
     diag_ref, cross_ref, mass_ref, raw, U, W, T, side, met, B, Br, Bc, Bd, inv,
-    sM, sA, sRB, sCA, sCB, rMc, rMr, rA, rRB, rCA, rCB, sent,
+    sM, sMd, sA, sRB, sCA, sCB, rMc, rMr, rMd, rA, rRB, rCA, rCB, sent,
     small_sem, load_sem, send_sem, recv_sem, late,
 ):
     face, col = lax.axis_index("face"), lax.axis_index("col")
@@ -180,8 +180,8 @@
         ).wait_recv()
 
     def row_metrics(s):
-        return [copy_of(3 + 3 * (1 - s), s, sM.at[s], rMr.at[1 - s, 0])] + [
-            copy_of(3 + 3 * (1 - s), 4 + 2 * s + t, sM.at[s], rMr.at[1 - s, 2 - t]) for t in range(2)
+        return [copy_of(3 + 3 * (1 - s), s, sM.at[s], rMr.at[1 - s])] + [
+            copy_of(9 + 1 - s, 4 + 2 * s + t, sMd.at[s, t], rMd.at[1 - s, 1 - t]) for t in range(2)
         ]
 
     def row_edges(s, at, size):
@@ -240,6 +240,14 @@
                 v = pltpu.roll(met[ex, half, :], (4 * ex - t * (ny - 4)) % lanes, 1)
                 packed[i] = jnp.where((lane >= 4 * ex) & (lane < 4 * ex + 4), v, packed[i])
         sM[2 + t] = side_by_side(*packed)
+    for s in range(2):
+        for t in range(2):
+            y, v = t * (ny - 4), sM[s]
+            v = jnp.where(
+                lane < 4, pltpu.roll(v, -y % lanes, 1), pltpu.roll(v, (4 - half_lanes - y) % lanes, 1)
+            )
+            v = pltpu.roll(jnp.where(lane < 8, v, 0.0), 0, 1, stride=8, stride_axis=0)
+            sMd[s, t] = jnp.sum(v, axis=0, keepdims=True)
 
     def inverted(ex, mass_of=lambda v: v):
         v = met[ex, halves_of[1], :]
@@ -535,7 +543,18 @@
     def ring_metrics(s):
         ex, own_row, halo_row = s * (nbx - 1), 3 * s, 3 - 3 * s
         arrived(3 + 3 * s, rMr.at[s])
-        beyond = [turned(rMr[s, k], -half_lanes) for k in range(3)]
+        arrived(9 + s, rMd.at[s])
+        theirs = [rMr[s]]
+        for t in range(2):
+            y = (1 - t) * (ny - 4)
+            row = wide(rMd[s, t])
+            v = row
+            for i in range(1, 8):
+                v = jnp.where(sub == i, turned(row, -8 * i), v)
+            theirs.append(jnp.where(
+                lane < half_lanes, turned(v, y), turned(v, half_lanes + y - 4)
+            ))
+        beyond = [turned(v, -half_lanes) for v in theirs]
         own = sub == 4 + own_row
         ends = [
             column_masses(t, ex)
@@ -547,9 +566,9 @@
         ))
         for y in range(ny):
             B[ex, y, halves_of[1], :] = in_all_lanes(v, y)
-        lift(rMr[s, 0], Br, (s,), range(ny))
-        for t in range(2):
-            lift(rMr[s, 1 + t], Bd, (2 * s + t,), range(4) if t else range(ny - 4, ny))
+        lift(theirs[0], Br, (s,), range(ny))
+        for t in range(2):
+            lift(theirs[1 + t], Bd, (2 * s + t,), range(4) if t else range(ny - 4, ny))
             v = 1.0 / (
                 mass_row(turned(rMc[t], -(half_lanes + 4 * ex)), own_row)
                 + mass_row(turned(beyond[1 + t], 0 if t else -(ny - 4)), halo_row)
@@ -672,7 +691,7 @@
                 vmem(2, nx // 2, 2 * nf, lanes),
             ]
 
-        tiles_sent = 2 * (2 * nq + 3 + 4) + 2 * (nx + 4) + 8 + 8
+        tiles_sent = 2 * (2 * nq + 3 + 4) + 2 * (nx + 4) + 8 + 4
         out = pl.pallas_call(
             functools.partial(kernel, faces, cols, nf, nbx, nby),
             out_shape=jax.ShapeDtypeStruct(tiles, f32),
@@ -694,15 +713,17 @@
                 vmem(4, 4, 16, lanes),
                 vmem(2, 7, 2 * nf, lanes),
                 vmem(4, 2 * nf, lanes),
+                vmem(2, 2, 1, lanes),
                 *messages(),
                 vmem(2, 2 * nf, lanes),
-                vmem(2, 3, 2 * nf, lanes),
+                vmem(2, 2 * nf, lanes),
+                vmem(2, 2, 1, lanes),
                 *messages(),
-                vmem(tiles_sent, 2 * nf, lanes),
+                vmem(tiles_sent * 2 * nf + 4, 1, lanes),
                 pltpu.SemaphoreType.DMA((3,)),
                 pltpu.SemaphoreType.DMA,
                 pltpu.SemaphoreType.DMA,
-                pltpu.SemaphoreType.DMA((9,)),
+                pltpu.SemaphoreType.DMA((11,)),
                 pltpu.SemaphoreType.REGULAR((2,)),
             ],
             compiler_params=pltpu.CompilerParams(

time: 12.9 us -> 12.8 us (level)
  no operation moved by 1% of the time
where the time goes in v6:
time: 12.8 us; the launch traced here: 12.7 us
  Pallas kernels  11.8 us (92%)
  local copies, waits for them, and re-layouts  0.89 us (7%)
    pallas_call x1, Pallas kernels, shards(): pl.pallas_call(functools.partial(kernel, faces, cols, nf, nbx, nby), out_...  11.8 us
    unnamed x1, local copies, waits for them, and re-layouts  0.89 us

profile of v6, /device:TPU:0, one launch (start us, length us, event | category | flops | bytes accessed | tf_op | source)
XLA Modules:
  0.0 12.7 jit_solution(11209800639110798682)
XLA Ops:
  0.0 11.8 %shard_map.46 = f32[20,10,8,128]{3,2,1,0:T(8,128)S(1)} custom-call(f32[20,10,8,128]{3,2,1,0:T(8,128)} %bitcast.8, f32[20,2,20]{2,1,0:T(2,128)} %bitcast.9, f32[20,20]{1,0:T(8,128)} %cross_hbm.1, f32[20,20]{1,0:T(8,128)} %mass_hbm.1), custom_call_target="tpu_custom_call" | custom-call | tf_op jit(solution)/shard_map/pallas_call | solution.py:695
  11.8 0.9 %copy.6 = f32[4,20,20,128]{3,0,2,1:T(4,128)} copy(f32[4,20,20,128]{3,0,2,1:T(4,128)S(1)} %bitcast.7) | data formatting | bytes 1638400
